TPU v7x, 512 devices: a whole 4x8x8 slice. The times are simulated.
512 devices in a mesh: band: 16 (over x, z_hi), fft: 32 (over y, z_lo, core).
Axes of the slice: x: 4, y: 8, z: 8 (z_hi: 4, z_lo: 2; z = z_hi * 2 + z_lo), core: 2. Of those that a mesh axis runs over, the one named last changes fastest.
Arguments:
- wave: float32 [2, 32, 128, 128, 128], P(None, 'band', 'fft'), may hold values from -6 to 6
- previous: float32 [2, 32, 128, 128, 128], P(None, 'band', 'fft'), may hold values from -6 to 6
- potential: float32 [128, 128, 128], P('band', 'fft'), may hold values from -1.5 to 1.5
- column_extent: int32 [128, 128], P('fft'), may hold values from -1 to 31, as said below
- metric: float32 [3], replicated, may hold values from 0.5 to 2
- center: float32 [1], replicated, may hold values from 0.5 to 2
- halfwidth: float32 [1], replicated, may hold values from 1 to 3
Outputs:
- filtered: float32 [2, 32, 128, 128, 128], P(None, 'band', 'fft')
Inputs may be any that keep to these rules, and one draw needn't show every extreme that they name: `column_extent`: every entry is -1 where |s(gx)| >= 32 or |s(gy)| >= 32, with s the signed index of the steps. Some column reaches the maximum.
All inputs are finite; a program needn't handle non-finite values.
Results may differ from a plain program's by a relative error of at most 0.00005.
Values sent between devices are 32-bit elements; how exact they have to be, the bound alone decides.
No kernel may reach another device: no remote copies, remote signals or barrier semaphores. Data moves between devices by JAX's collectives and lax.ppermute only.
A program may use at most 64 MiB of HBM per device.

v0:
```python
import math

import jax
import jax.numpy as jnp
import numpy as np
from jax import lax
from jax.experimental import pallas as pl
from jax.experimental.pallas import tpu as pltpu
from jax.sharding import PartitionSpec as P

N = 128
H = 32
K = 2 * H
F32 = jnp.float32
BF16 = jnp.bfloat16


def kept():
    g = np.arange(K)
    return np.where(g < H, g, g + N - K)


def angles(rows, cols):
    return 2.0 * math.pi * ((rows[:, None] * cols[None, :]) % N) / N


def lanes():
    g = np.concatenate([np.arange(H), np.arange(N - H, N), np.arange(H), np.arange(N - H, N)])
    imag = np.repeat([0, 1, 1, 0], H)
    return g, imag


def split_table(table):
    hi = table.astype(np.float32).astype(BF16)
    lo = (table - hi.astype(np.float64)).astype(np.float32).astype(BF16)
    return hi, lo


def z_inverse_table():
    theta = angles(np.arange(N), kept())
    both = np.concatenate([np.cos(theta), np.sin(theta)], axis=1)
    out = np.zeros((N // 4, 2, 4, 2, 2 * K))
    for b in range(2):
        out[:, b, :, b, :] = both.reshape(N // 4, 4, 2 * K)
    return out.reshape(2 * N, 4 * K)


def z_forward_table():
    theta = angles(kept(), np.arange(N))
    out = np.zeros((2, 2, K, N // 4, 2, 4))
    for b in range(2):
        out[0, b, :, :, b, :] = np.cos(theta).reshape(K, N // 4, 4) / N
        out[1, b, :, :, b, :] = np.sin(theta).reshape(K, N // 4, 4) / N
    return out.reshape(4 * K, 2 * N)


def y_inverse_table():
    g, imag = lanes()
    theta = angles(g, np.arange(N))
    re = np.where(imag[:, None] == 0, np.cos(theta), -np.sin(theta))
    im = np.where(imag[:, None] == 0, np.sin(theta), np.cos(theta))
    return np.concatenate([re, im], axis=1)


def y_forward_table():
    g, imag = lanes()
    theta = angles(np.arange(N), g)
    re = np.where(imag[None, :] == 0, np.cos(theta), -np.sin(theta))
    im = np.where(imag[None, :] == 0, np.sin(theta), np.cos(theta))
    return np.concatenate([re, im], axis=0) / N


def x_inverse_table():
    theta = angles(np.arange(N), kept())
    c, s = np.cos(theta), np.sin(theta)
    return np.block([[c, -s], [s, c]])


def x_forward_table():
    theta = angles(kept(), np.arange(N))
    c, s = np.cos(theta), np.sin(theta)
    return np.block([[c, s], [-s, c]]) / N


def split(value):
    hi = value.astype(BF16)
    return hi, (value - hi.astype(F32)).astype(BF16)


def mm(a, b):
    return jnp.dot(a, b, preferred_element_type=F32)


def outer_lanes(shape):
    lane = lax.broadcasted_iota(jnp.int32, shape, 1)
    return (lane < H) | (lane >= N - H)


def kept_abs(shape):
    row = lax.broadcasted_iota(jnp.int32, shape, 0)
    return jnp.where(row < H, row, K - row)


def kept_rows(ref, *index):
    return jnp.concatenate([ref[(*index, slice(0, H))], ref[(*index, slice(N - H, N))]], axis=0)


def z_inverse_kernel(
    wave_hbm, extent_hbm, th_hbm, tl_hbm, o_ref, wave_ref, extent_ref, th_ref, tl_ref, sems
):
    copies = [
        pltpu.make_async_copy(extent_hbm, extent_ref, sems.at[0]),
        pltpu.make_async_copy(
            wave_hbm.at[:, :, :, 0:H, :], wave_ref.at[:, :, :, 0:H, :], sems.at[1]
        ),
        pltpu.make_async_copy(
            wave_hbm.at[:, :, :, N - H : N, :], wave_ref.at[:, :, :, H:K, :], sems.at[2]
        ),
        pltpu.make_async_copy(th_hbm, th_ref, sems.at[3]),
        pltpu.make_async_copy(tl_hbm, tl_ref, sems.at[4]),
    ]
    for copy in copies:
        copy.start()
    outer = outer_lanes((K, N))
    sign = jnp.where(outer, -1.0, 1.0)
    size = kept_abs((K, N))
    for copy in copies:
        copy.wait()
    for gx in range(4):
        keep = size <= extent_ref[gx : gx + 1, :]
        rows = []
        for b in range(2):
            re = jnp.where(keep, wave_ref[0, b, gx], 0.0)
            im = jnp.where(keep, wave_ref[1, b, gx], 0.0)
            x = jnp.where(outer, re, pltpu.roll(im, N // 2, 1))
            rows += [x, pltpu.roll(x, N // 2, 1) * sign]
        hi, lo = split(jnp.concatenate(rows, axis=0))
        out = mm(th_ref[...], hi) + mm(th_ref[...], lo) + mm(tl_ref[...], hi)
        o_ref[:, 8 * gx : 8 * gx + 8, :] = out.reshape(N // 4, 8, N)


def middle_kernel(
    r_ref, near_ref, far_ref, yi_ref, yil_ref, xi_ref, xil_ref, xf_ref, xfl_ref, yf_ref, yfl_ref, o_ref
):
    band = lax.axis_index("band")
    my_x, my_z = band // 4, band % 4
    v = []
    for z in range(4):
        parts = []
        for j in range(16):
            dx, dz = my_x ^ (j // 4), my_z ^ (j % 4)
            slot = (dx ^ (dx // 2)) * 4 + (dz ^ (dz // 2))
            start = (slot % 8) * 32 + z
            parts.append(
                jnp.where(
                    slot < 8,
                    near_ref[pl.ds(start, 8, stride=4), :],
                    far_ref[pl.ds(start, 8, stride=4), :],
                )
            )
        v.append(jnp.concatenate(parts, axis=0))
    for z in range(4):
        rows = []
        for p in (z, 4 + z):
            rows += [r_ref[pl.ds(p, H, stride=8), :], r_ref[pl.ds(8 * (N - H) + p, H, stride=8), :]]
        hi, lo = split(jnp.concatenate(rows, axis=0))
        y = mm(hi, yi_ref[...]) + mm(lo, yi_ref[...]) + mm(hi, yil_ref[...])
        f = jnp.concatenate(
            [
                jnp.concatenate([y[:K, :N], y[:K, N:]], axis=0),
                jnp.concatenate([y[K:, :N], y[K:, N:]], axis=0),
            ],
            axis=1,
        )
        hi, lo = split(f)
        s = mm(xi_ref[...], hi) + mm(xi_ref[...], lo) + mm(xil_ref[...], hi)
        vz = jnp.concatenate([v[z], v[z]], axis=0)
        s = s * jnp.concatenate([vz, vz], axis=1)
        hi, lo = split(s)
        g = mm(xf_ref[...], hi) + mm(xf_ref[...], lo) + mm(xfl_ref[...], hi)
        rows = jnp.concatenate(
            [
                jnp.concatenate([g[:K, :N], g[K:, :N]], axis=1),
                jnp.concatenate([g[:K, N:], g[K:, N:]], axis=1),
            ],
            axis=0,
        )
        hi, lo = split(rows)
        out = mm(hi, yf_ref[...]) + mm(lo, yf_ref[...]) + mm(hi, yfl_ref[...])
        for b in range(2):
            p = 4 * b + z
            o_ref[pl.ds(p, H, stride=8), :] = out[b * K : b * K + H]
            o_ref[pl.ds(8 * (N - H) + p, H, stride=8), :] = out[b * K + H : b * K + K]
    o_ref[8 * H : 8 * (N - H), :] = jnp.zeros((8 * (N - K), N), F32)


def update_kernel(
    r_ref, wave_ref, previous_ref, extent_ref, zh_ref, zl_ref, metric_ref, center_ref, half_ref, o_ref
):
    outer = outer_lanes((K, N))
    sign = jnp.where(outer, -1.0, 1.0)
    size = kept_abs((K, N))
    two_pi = 2.0 * math.pi
    lane = lax.broadcasted_iota(jnp.int32, (K, N), 1)
    signed_y = jnp.where(lane < N // 2, lane, lane - N)
    kinetic_y = (two_pi * signed_y.astype(F32) / N) ** 2
    kinetic_z = (two_pi * size.astype(F32) / N) ** 2
    factor = 2.0 / half_ref[0]
    center = center_ref[0]
    zeros = jnp.zeros((N - K, N), F32)
    for gx in range(4):
        hi, lo = split(r_ref[:, 8 * gx : 8 * gx + 8, :].reshape(2 * N, N))
        pq = mm(zh_ref[...], hi) + mm(zh_ref[...], lo) + mm(zl_ref[...], hi)
        keep = size <= extent_ref[gx : gx + 1, :]
        index_x = jnp.full((K, N), lax.axis_index("fft") * 4 + gx, jnp.int32)
        signed_x = jnp.where(index_x < N // 2, index_x, index_x - N)
        kinetic_x = (two_pi * signed_x.astype(F32) / N) ** 2
        kinetic = 0.5 * (
            metric_ref[0] * kinetic_x + metric_ref[2] * kinetic_z + metric_ref[1] * kinetic_y
        )
        for b in range(2):
            p, q = pq[b * K : b * K + K], pq[2 * K + b * K : 2 * K + b * K + K]
            applied = p - pltpu.roll(q, N // 2, 1) * sign
            for part, term in ((0, applied), (1, pltpu.roll(applied, N // 2, 1))):
                c = kept_rows(wave_ref, part, b, gx)
                value = factor * (kinetic * c + term - center * c) - kept_rows(
                    previous_ref, part, b, gx
                )
                value = jnp.where(keep, value, 0.0)
                o_ref[part, b, gx, 0:H, :] = value[:H]
                o_ref[part, b, gx, H : N - H, :] = zeros
                o_ref[part, b, gx, N - H : N, :] = value[H:]


VMEM = pl.BlockSpec(memory_space=pltpu.VMEM)
SMEM = pl.BlockSpec(memory_space=pltpu.SMEM)
HBM = pl.BlockSpec(memory_space=pltpu.HBM)


def call(kernel, shape, specs, flops, scratch=()):
    return pl.pallas_call(
        kernel,
        out_shape=jax.ShapeDtypeStruct(shape, F32),
        in_specs=specs,
        out_specs=VMEM,
        scratch_shapes=list(scratch),
        cost_estimate=pl.CostEstimate(flops=flops, bytes_accessed=2 << 20, transcendentals=0),
        compiler_params=pltpu.CompilerParams(vmem_limit_bytes=16 << 20),
    )


def swap(blocks):
    return lax.all_to_all(blocks, "fft", split_axis=0, concat_axis=0, tiled=True)


def exchange(value, dx, dz):
    pairs = [(i, (i // 4 ^ dx) * 4 + (i % 4 ^ dz)) for i in range(16)]
    return lax.ppermute(value, "band", pairs)


def gather_potential(potential):
    near = potential.reshape(32, N)
    for dx, dz in ((0, 1), (0, 3), (1, 0)):
        near = jnp.concatenate([near, exchange(near, dx, dz)], axis=0)
    return near, exchange(near, 3, 0)


def local(wave, previous, potential, column_extent, metric, center, halfwidth):
    zi, zf = split_table(z_inverse_table()), split_table(z_forward_table())
    yi, yf = split_table(y_inverse_table()), split_table(y_forward_table())
    xi, xf = split_table(x_inverse_table()), split_table(x_forward_table())
    near, far = gather_potential(potential)
    scratch = [
        pltpu.VMEM((2, 2, 4, K, N), F32),
        pltpu.VMEM((4, N), jnp.int32),
        pltpu.VMEM((2 * N, 4 * K), BF16),
        pltpu.VMEM((2 * N, 4 * K), BF16),
        pltpu.SemaphoreType.DMA((5,)),
    ]
    blocks = call(z_inverse_kernel, (32, 32, N), [HBM] * 4, 200_000_000, scratch)(
        wave, column_extent, *zi
    )
    blocks = swap(blocks).reshape(1024, N)
    blocks = call(middle_kernel, (1024, N), [VMEM] * 11, 800_000_000)(
        blocks, near, far, *yi, *xi, *xf, *yf
    )
    blocks = swap(blocks.reshape(32, 32, N))
    return call(update_kernel, wave.shape, [VMEM] * 6 + [SMEM] * 3, 200_000_000)(
        blocks, wave, previous, column_extent, *zf, metric, center, halfwidth
    )


def solution(mesh):
    in_specs = (
        P(None, "band", "fft", None, None),
        P(None, "band", "fft", None, None),
        P("band", "fft", None),
        P("fft", None),
        P(),
        P(),
        P(),
    )
    out_specs = P(None, "band", "fft", None, None)
    return jax.shard_map(local, mesh=mesh, in_specs=in_specs, out_specs=out_specs, check_vma=False)
```

profile of v0, /device:TPU:1, one launch (start us, length us, event | category | flops | bytes accessed | tf_op | source)
XLA Modules:
  0.0 81.5 jit_solution(18276488785950979865)
XLA Ops:
  0.0 0.0 copy-start
  0.0 1.2 %copy-done = f32[2,2,4,128,128]{4,3,2,1,0:T(8,128)S(1)} copy-done((f32[2,2,4,128,128]{4,3,2,1,0:T(8,128)S(1)}, f32[2,2,4,128,128]{4,3,2,1,0:T(8,128)}, u32[]{:S(2)}) %copy-start) | copy-done | bytes 1048600
  1.2 0.0 copy-start.5
  1.2 0.9 %copy-done.5 = bf16[256,256]{1,0:T(8,128)(2,1)S(1)} copy-done((bf16[256,256]{1,0:T(8,128)(2,1)S(1)}, bf16[256,256]{1,0:T(8,128)(2,1)}, u32[]{:S(2)}) %copy-start.5) | copy-done | bytes 131096
  2.1 0.0 copy-start.6
  2.1 0.9 %copy-done.6 = bf16[256,256]{1,0:T(8,128)(2,1)S(1)} copy-done((bf16[256,256]{1,0:T(8,128)(2,1)S(1)}, bf16[256,256]{1,0:T(8,128)(2,1)}, u32[]{:S(2)}) %copy-start.6) | copy-done | bytes 131096
  3.0 0.0 copy-start.7
  3.0 0.7 copy-done.7
  3.7 1.9 %shard_map.181 = f32[32,32,128]{2,1,0:T(8,128)} custom-call(f32[2,2,4,128,128]{4,3,2,1,0:T(8,128)S(1)} %copy-done, s32[4,128]{1,0:T(4,128)S(1)} %copy-done.7, bf16[256,256]{1,0:T(8,128)(2,1)S(1)} %copy-done.6, bf16[256,256]{1,0:T(8,128)(2,1)S(1)} %copy-done.5), custom_call_target="tpu_custom_call" | custom-call | flops 200000000 | bytes 2097152 | tf_op jit(solution)/shard_map/pallas_call | solution.py:280
  5.7 0.0 copy-start.18
  5.7 0.0 copy-start.17
  5.7 10.7 %all-to-all-start = ((f32[32,32,128]{2,1,0:T(8,128)}), f32[32,32,128]{2,1,0:T(8,128)S(1)}, u32[]{:S(2)}, u32[]{:S(2)}) async-start(f32[32,32,128]{2,1,0:T(8,128)} %shard_map.181), calls=%async_computation | async-start | bytes 1048576 | tf_op jit(solution)/shard_map/all_to_all | solution.py:253
  16.4 0.0 copy-done.18
  16.4 5.8 %collective-permute-start = (f32[32,128]{1,0:T(8,128)S(1)}, f32[32,128]{1,0:T(8,128)S(1)}, u32[]{:S(2)}, u32[]{:S(2)}) collective-permute-start(f32[32,128]{1,0:T(8,128)S(1)} %bitcast.4), channel_id=1, source_target_pairs={{0,32},{32,0},{64,96},{96,64},{128,160},{160,128},{192,224},{224,1... | collective-permute-start | bytes 49160 | tf_op jit(solution)/shard_map/ppermute | solution.py:258
  22.2 1.4 %collective-permute-done = f32[32,128]{1,0:T(8,128)S(1)} collective-permute-done((f32[32,128]{1,0:T(8,128)S(1)}, f32[32,128]{1,0:T(8,128)S(1)}, u32[]{:S(2)}, u32[]{:S(2)}) %collective-permute-start) | collective-permute-done | bytes 16416 | tf_op jit(solution)/shard_map/ppermute | solution.py:258
  23.6 0.0 copy-start.16
  23.6 9.5 %collective-permute-start.1 = (f32[64,128]{1,0:T(8,128)S(1)}, f32[64,128]{1,0:T(8,128)S(1)}, u32[]{:S(2)}, u32[]{:S(2)}) collective-permute-start(f32[64,128]{1,0:T(8,128)S(1)} %pad_maximum_fusion.2), channel_id=1, source_target_pairs={{0,96},{32,64},{64,32},{96,0},{128,224},{160,192},{192,160},{224,1... | collective-permute-start | bytes 98312 | tf_op jit(solution)/shard_map/ppermute | solution.py:258
  33.1 1.4 %collective-permute-done.1 = f32[64,128]{1,0:T(8,128)S(1)} collective-permute-done((f32[64,128]{1,0:T(8,128)S(1)}, f32[64,128]{1,0:T(8,128)S(1)}, u32[]{:S(2)}, u32[]{:S(2)}) %collective-permute-start.1) | collective-permute-done | bytes 32800 | tf_op jit(solution)/shard_map/ppermute | solution.py:258
  34.6 0.0 copy-start.14
  34.6 0.0 copy-start.15
  34.6 0.0 copy-start.10
  34.6 0.0 copy-start.11
  34.6 0.0 copy-start.12
  34.6 0.0 copy-start.13
  34.6 3.3 %collective-permute-start.2 = (f32[128,128]{1,0:T(8,128)S(1)}, f32[128,128]{1,0:T(8,128)S(1)}, u32[]{:S(2)}, u32[]{:S(2)}) collective-permute-start(f32[128,128]{1,0:T(8,128)S(1)} %pad_maximum_fusion.1), channel_id=1, source_target_pairs={{0,128},{32,160},{64,192},{96,224},{128,0},{160,32},{192,64},{224,... | collective-permute-start | bytes 196616 | tf_op jit(solution)/shard_map/ppermute | solution.py:258
  37.9 1.9 %collective-permute-done.2 = f32[128,128]{1,0:T(8,128)S(1)} collective-permute-done((f32[128,128]{1,0:T(8,128)S(1)}, f32[128,128]{1,0:T(8,128)S(1)}, u32[]{:S(2)}, u32[]{:S(2)}) %collective-permute-start.2) | collective-permute-done | bytes 65568 | tf_op jit(solution)/shard_map/ppermute | solution.py:258
  39.8 4.4 %collective-permute-start.3 = (f32[256,128]{1,0:T(8,128)S(1)}, f32[256,128]{1,0:T(8,128)S(1)}, u32[]{:S(2)}, u32[]{:S(2)}) collective-permute-start(f32[256,128]{1,0:T(8,128)S(1)} %pad_maximum_fusion.near_ref), channel_id=1, source_target_pairs={{0,384},{32,416},{64,448},{96,480},{128,256},{160,288},{192,320},{... | collective-permute-start | bytes 393224 | tf_op jit(solution)/shard_map/ppermute | solution.py:258
  44.2 2.5 %collective-permute-done.3.far_ref = f32[256,128]{1,0:T(8,128)S(1)} collective-permute-done((f32[256,128]{1,0:T(8,128)S(1)}, f32[256,128]{1,0:T(8,128)S(1)}, u32[]{:S(2)}, u32[]{:S(2)}) %collective-permute-start.3) | collective-permute-done | bytes 131104 | tf_op jit(solution)/shard_map/ppermute | solution.py:258
  46.7 0.0 all-to-all-done
  46.7 0.0 copy-done.17
  46.7 0.0 copy-done.16
  46.7 0.0 copy-done.14
  46.7 0.0 copy-done.15
  46.7 0.0 copy-done.10
  46.7 0.0 copy-done.11
  46.8 0.0 copy-done.12
  46.8 0.0 copy-done.13
  46.8 0.0 copy-start.2
  46.8 0.0 copy-start.3
  46.8 0.0 copy-start.4
  46.8 4.2 %shard_map.182 = f32[1024,128]{1,0:T(8,128)} custom-call(f32[1024,128]{1,0:T(8,128)S(1)} %bitcast.3, f32[256,128]{1,0:T(8,128)S(1)} %pad_maximum_fusion.near_ref, f32[256,128]{1,0:T(8,128)S(1)} %collective-permute-done.3.far_ref, bf16[128,256]{1,0:T(8,128)(2,1)S(1)} %copy-done.17, bf16[128,256]{1,0:T(8,128)(2,1)S(1)} %copy-done.16, ...), custom_call_target="tpu_custom_call" | custom-call | flops 800000000 | bytes 2097152 | tf_op jit(solution)/shard_map/pallas_call | solution.py:284
  51.0 0.0 copy-start.1
  51.0 11.6 %all-to-all-start.1 = ((f32[32,32,128]{2,1,0:T(8,128)}), f32[32,32,128]{2,1,0:T(8,128)S(1)}, u32[]{:S(2)}, u32[]{:S(2)}) async-start(f32[32,32,128]{2,1,0:T(8,128)} %bitcast.2), calls=%async_computation.1 | async-start | bytes 1048576 | tf_op jit(solution)/shard_map/all_to_all | solution.py:253
  62.7 0.0 copy-start.8
  63.3 0.0 copy-start.9
  64.0 15.2 %all-to-all-done.1.r_ref = f32[32,32,128]{2,1,0:T(8,128)S(1)} async-done(((f32[32,32,128]{2,1,0:T(8,128)}), f32[32,32,128]{2,1,0:T(8,128)S(1)}, u32[]{:S(2)}, u32[]{:S(2)}) %all-to-all-start.1) | async-done | bytes 524320 | tf_op jit(solution)/shard_map/all_to_all | solution.py:253
  79.2 0.0 copy-done.2
  79.2 0.0 copy-done.3
  79.2 0.0 copy-done.4
  79.2 0.0 copy-done.1
  79.2 0.0 copy-done.8
  79.2 0.0 copy-done.9
  79.3 2.2 %shard_map.183 = f32[2,2,4,128,128]{4,3,2,1,0:T(8,128)} custom-call(f32[32,32,128]{2,1,0:T(8,128)S(1)} %all-to-all-done.1.r_ref, f32[2,2,4,128,128]{4,3,2,1,0:T(8,128)S(1)} %copy-done.1, f32[2,2,4,128,128]{4,3,2,1,0:T(8,128)S(1)} %copy-done.2, s32[4,128]{1,0:T(4,128)S(1)} %copy-done.8, bf16[256,256]{1,0:T(8,128)(2,1)S(1)} %copy-done.4, ...), custom_call_target="tpu_custom_call" | custom-call | flops 200000000 | bytes 2097152 | tf_op jit(solution)/shard_map/pallas_call | solution.py:288
  (3 shorter events, 0.0 us)
Async XLA Ops:
  0.0 1.2 %copy-start = (f32[2,2,4,128,128]{4,3,2,1,0:T(8,128)S(1)}, f32[2,2,4,128,128]{4,3,2,1,0:T(8,128)}, u32[]{:S(2)}) copy-start(f32[2,2,4,128,128]{4,3,2,1,0:T(8,128)} %wave_ref.1) | copy-start | bytes 3145732
  1.2 0.9 %copy-start.5 = (bf16[256,256]{1,0:T(8,128)(2,1)S(1)}, bf16[256,256]{1,0:T(8,128)(2,1)}, u32[]{:S(2)}) copy-start(bf16[256,256]{1,0:T(8,128)(2,1)} %constant.25.clone.tl_hbm) | copy-start | bytes 393220
  2.1 0.9 %copy-start.6 = (bf16[256,256]{1,0:T(8,128)(2,1)S(1)}, bf16[256,256]{1,0:T(8,128)(2,1)}, u32[]{:S(2)}) copy-start(bf16[256,256]{1,0:T(8,128)(2,1)} %constant.24.clone.th_hbm) | copy-start | bytes 393220
  3.0 0.7 copy-start.7
  5.7 10.7 %copy-start.18 = (f32[8,4,128]{2,1,0:T(4,128)S(1)}, f32[8,4,128]{2,1,0:T(4,128)}, u32[]{:S(2)}) copy-start(f32[8,4,128]{2,1,0:T(4,128)} %param.21) | copy-start | bytes 49156
  5.7 41.0 %copy-start.17 = (bf16[128,256]{1,0:T(8,128)(2,1)S(1)}, bf16[128,256]{1,0:T(8,128)(2,1)}, u32[]{:S(2)}) copy-start(bf16[128,256]{1,0:T(8,128)(2,1)} %constant.26.clone.yi_ref) | copy-start | bytes 196612
  5.7 41.0 %all-to-all-start = ((f32[32,32,128]{2,1,0:T(8,128)}), f32[32,32,128]{2,1,0:T(8,128)S(1)}, u32[]{:S(2)}, u32[]{:S(2)}) async-start(f32[32,32,128]{2,1,0:T(8,128)} %shard_map.181), calls=%async_computation | async-start | bytes 1048576 | tf_op jit(solution)/shard_map/all_to_all | solution.py:253
  16.4 7.2 %collective-permute-start = (f32[32,128]{1,0:T(8,128)S(1)}, f32[32,128]{1,0:T(8,128)S(1)}, u32[]{:S(2)}, u32[]{:S(2)}) collective-permute-start(f32[32,128]{1,0:T(8,128)S(1)} %bitcast.4), channel_id=1, source_target_pairs={{0,32},{32,0},{64,96},{96,64},{128,160},{160,128},{192,224},{224,1... | collective-permute-start | bytes 49160 | tf_op jit(solution)/shard_map/ppermute | solution.py:258
  23.6 23.1 %copy-start.16 = (bf16[128,256]{1,0:T(8,128)(2,1)S(1)}, bf16[128,256]{1,0:T(8,128)(2,1)}, u32[]{:S(2)}) copy-start(bf16[128,256]{1,0:T(8,128)(2,1)} %constant.27.clone.yil_ref) | copy-start | bytes 196612
  23.6 10.9 %collective-permute-start.1 = (f32[64,128]{1,0:T(8,128)S(1)}, f32[64,128]{1,0:T(8,128)S(1)}, u32[]{:S(2)}, u32[]{:S(2)}) collective-permute-start(f32[64,128]{1,0:T(8,128)S(1)} %pad_maximum_fusion.2), channel_id=1, source_target_pairs={{0,96},{32,64},{64,32},{96,0},{128,224},{160,192},{192,160},{224,1... | collective-permute-start | bytes 98312 | tf_op jit(solution)/shard_map/ppermute | solution.py:258
  34.6 12.2 %copy-start.14 = (bf16[256,128]{1,0:T(8,128)(2,1)S(1)}, bf16[256,128]{1,0:T(8,128)(2,1)}, u32[]{:S(2)}) copy-start(bf16[256,128]{1,0:T(8,128)(2,1)} %constant.29.clone.xil_ref) | copy-start | bytes 196612
  34.6 12.2 %copy-start.15 = (bf16[256,128]{1,0:T(8,128)(2,1)S(1)}, bf16[256,128]{1,0:T(8,128)(2,1)}, u32[]{:S(2)}) copy-start(bf16[256,128]{1,0:T(8,128)(2,1)} %constant.28.clone.xi_ref) | copy-start | bytes 196612
  34.6 12.2 %copy-start.10 = (bf16[256,128]{1,0:T(8,128)(2,1)S(1)}, bf16[256,128]{1,0:T(8,128)(2,1)}, u32[]{:S(2)}) copy-start(bf16[256,128]{1,0:T(8,128)(2,1)} %constant.33.clone.yfl_ref) | copy-start | bytes 196612
  34.6 12.2 %copy-start.11 = (bf16[256,128]{1,0:T(8,128)(2,1)S(1)}, bf16[256,128]{1,0:T(8,128)(2,1)}, u32[]{:S(2)}) copy-start(bf16[256,128]{1,0:T(8,128)(2,1)} %constant.32.clone.yf_ref) | copy-start | bytes 196612
  34.6 12.2 %copy-start.12 = (bf16[128,256]{1,0:T(8,128)(2,1)S(1)}, bf16[128,256]{1,0:T(8,128)(2,1)}, u32[]{:S(2)}) copy-start(bf16[128,256]{1,0:T(8,128)(2,1)} %constant.31.clone.xfl_ref) | copy-start | bytes 196612
  34.6 12.2 %copy-start.13 = (bf16[128,256]{1,0:T(8,128)(2,1)S(1)}, bf16[128,256]{1,0:T(8,128)(2,1)}, u32[]{:S(2)}) copy-start(bf16[128,256]{1,0:T(8,128)(2,1)} %constant.30.clone.xf_ref) | copy-start | bytes 196612
  34.6 5.1 %collective-permute-start.2 = (f32[128,128]{1,0:T(8,128)S(1)}, f32[128,128]{1,0:T(8,128)S(1)}, u32[]{:S(2)}, u32[]{:S(2)}) collective-permute-start(f32[128,128]{1,0:T(8,128)S(1)} %pad_maximum_fusion.1), channel_id=1, source_target_pairs={{0,128},{32,160},{64,192},{96,224},{128,0},{160,32},{192,64},{224,... | collective-permute-start | bytes 196616 | tf_op jit(solution)/shard_map/ppermute | solution.py:258
  39.8 6.9 %collective-permute-start.3 = (f32[256,128]{1,0:T(8,128)S(1)}, f32[256,128]{1,0:T(8,128)S(1)}, u32[]{:S(2)}, u32[]{:S(2)}) collective-permute-start(f32[256,128]{1,0:T(8,128)S(1)} %pad_maximum_fusion.near_ref), channel_id=1, source_target_pairs={{0,384},{32,416},{64,448},{96,480},{128,256},{160,288},{192,320},{... | collective-permute-start | bytes 393224 | tf_op jit(solution)/shard_map/ppermute | solution.py:258
  46.8 32.4 %copy-start.2 = (f32[2,2,4,128,128]{4,3,2,1,0:T(8,128)S(1)}, f32[2,2,4,128,128]{4,3,2,1,0:T(8,128)}, u32[]{:S(2)}) copy-start(f32[2,2,4,128,128]{4,3,2,1,0:T(8,128)} %previous_ref.1) | copy-start | bytes 3145732
  46.8 32.4 %copy-start.3 = (bf16[256,256]{1,0:T(8,128)(2,1)S(1)}, bf16[256,256]{1,0:T(8,128)(2,1)}, u32[]{:S(2)}) copy-start(bf16[256,256]{1,0:T(8,128)(2,1)} %constant.35.clone.zl_ref) | copy-start | bytes 393220
  46.8 32.4 %copy-start.4 = (bf16[256,256]{1,0:T(8,128)(2,1)S(1)}, bf16[256,256]{1,0:T(8,128)(2,1)}, u32[]{:S(2)}) copy-start(bf16[256,256]{1,0:T(8,128)(2,1)} %constant.34.clone.zh_ref) | copy-start | bytes 393220
  51.0 28.2 %copy-start.1 = (f32[2,2,4,128,128]{4,3,2,1,0:T(8,128)S(1)}, f32[2,2,4,128,128]{4,3,2,1,0:T(8,128)}, u32[]{:S(2)}) copy-start(f32[2,2,4,128,128]{4,3,2,1,0:T(8,128)} %wave_ref.1) | copy-start | bytes 3145732
  51.0 28.2 %all-to-all-start.1 = ((f32[32,32,128]{2,1,0:T(8,128)}), f32[32,32,128]{2,1,0:T(8,128)S(1)}, u32[]{:S(2)}, u32[]{:S(2)}) async-start(f32[32,32,128]{2,1,0:T(8,128)} %bitcast.2), calls=%async_computation.1 | async-start | bytes 1048576 | tf_op jit(solution)/shard_map/all_to_all | solution.py:253
  62.7 16.6 %copy-start.8 = (s32[4,128]{1,0:T(4,128)S(1)}, s32[4,128]{1,0:T(4,128)}, u32[]{:S(2)}) copy-start(s32[4,128]{1,0:T(4,128)} %extent_ref.1) | copy-start | bytes 6148
  63.3 15.9 %copy-start.9 = (f32[3]{0:T(128)S(1)}, f32[3]{0:T(128)}, u32[]{:S(2)}) copy-start(f32[3]{0:T(128)} %metric_ref.1) | copy-start | bytes 40
where the time goes:
time: 82.1 us; the launch traced here: 81.5 us
  starting transfers between devices  45.3 us (55%)
  waiting for transfers between devices  22.5 us (27%)
  Pallas kernels  8.37 us (10%)
  local copies, waits for them, and re-layouts  3.8 us (5%)
  between operations  1.56 us (2%)
    ppermute x4, starting transfers between devices, exchange(): return lax.ppermute(value, 'band', pairs)  22.9 us
    all_to_all x2, starting transfers between devices, swap(): lax.all_to_all(blocks, 'fft', split_axis=0, concat_axis=0, tiled=True)  22.3 us
    all_to_all x2, waiting for transfers between devices, swap(): lax.all_to_all(blocks, 'fft', split_axis=0, concat_axis=0, tiled=True)  15.2 us
    ppermute x4, waiting for transfers between devices, exchange(): return lax.ppermute(value, 'band', pairs)  7.25 us
    pallas_call x1, Pallas kernels, local(): call(middle_kernel, (1024, N), [VMEM] * 11, 800000000)  4.2 us
    unnamed x38, local copies, waits for them, and re-layouts  3.8 us
    pallas_call x1, Pallas kernels, local(): call(update_kernel, wave.shape, [VMEM] * 6 + [SMEM] * 3, 200000000)  2.24 us
    pallas_call x1, Pallas kernels, local(): call(z_inverse_kernel, (32, 32, N), [HBM] * 4, 200000000, scratch)  1.94 us
  transfers between devices with their start and end apart: 6, of which 5 were waited for; matrix products, arithmetic and copies ran while one was open for 0% of the time, Pallas kernels for 0%

commit v1 on v0

--- a/solution.py
+++ b/solution.py
@@ -139,32 +139,30 @@
         o_ref[:, 8 * gx : 8 * gx + 8, :] = out.reshape(N // 4, 8, N)
 
 
-def middle_kernel(
-    r_ref, near_ref, far_ref, yi_ref, yil_ref, xi_ref, xil_ref, xf_ref, xfl_ref, yf_ref, yfl_ref, o_ref
+def inverse_kernel(
+    r_ref,
+    yi_ref,
+    yil_ref,
+    xi_ref,
+    xil_ref,
+    extent_ref,
+    metric_ref,
+    center_ref,
+    half_ref,
+    s_ref,
+    aux_ref,
 ):
-    band = lax.axis_index("band")
-    my_x, my_z = band // 4, band % 4
-    v = []
-    for z in range(4):
-        parts = []
-        for j in range(16):
-            dx, dz = my_x ^ (j // 4), my_z ^ (j % 4)
-            slot = (dx ^ (dx // 2)) * 4 + (dz ^ (dz // 2))
-            start = (slot % 8) * 32 + z
-            parts.append(
-                jnp.where(
-                    slot < 8,
-                    near_ref[pl.ds(start, 8, stride=4), :],
-                    far_ref[pl.ds(start, 8, stride=4), :],
-                )
-            )
-        v.append(jnp.concatenate(parts, axis=0))
+    aux_ref[0:4, :] = extent_ref[...].astype(F32)
+    row = lax.broadcasted_iota(jnp.int32, (4, N), 0)
+    metric = jnp.where(row == 1, metric_ref[0], jnp.where(row == 2, metric_ref[1], metric_ref[2]))
+    aux_ref[4:8, :] = jnp.where(row == 0, center_ref[0], metric)
+    aux_ref[8:16, :] = jnp.full((8, N), 2.0 / half_ref[0], F32)
     for z in range(4):
         rows = []
         for p in (z, 4 + z):
             rows += [r_ref[pl.ds(p, H, stride=8), :], r_ref[pl.ds(8 * (N - H) + p, H, stride=8), :]]
         hi, lo = split(jnp.concatenate(rows, axis=0))
-        y = mm(hi, yi_ref[...]) + mm(lo, yi_ref[...]) + mm(hi, yil_ref[...])
+        y = mm(jnp.concatenate([hi, lo], axis=1), yi_ref[...]) + mm(hi, yil_ref[...])
         f = jnp.concatenate(
             [
                 jnp.concatenate([y[:K, :N], y[:K, N:]], axis=0),
@@ -173,9 +171,26 @@
             axis=1,
         )
         hi, lo = split(f)
-        s = mm(xi_ref[...], hi) + mm(xi_ref[...], lo) + mm(xil_ref[...], hi)
-        vz = jnp.concatenate([v[z], v[z]], axis=0)
-        s = s * jnp.concatenate([vz, vz], axis=1)
+        s = mm(xi_ref[...], jnp.concatenate([hi, lo], axis=0)) + mm(xil_ref[...], hi)
+        s_ref[:, 2 * N * z : 2 * N * (z + 1)] = s
+
+
+def forward_kernel(
+    s_ref, v0_ref, v1_ref, v3_ref, v2_ref, xf_ref, xfl_ref, yf_ref, o_ref, v_ref
+):
+    band = lax.axis_index("band")
+    my_x, my_z = band // 4, band % 4
+    for dz, ref in ((0, v0_ref), (1, v1_ref), (3, v3_ref), (2, v2_ref)):
+        v_ref[pl.ds(pl.multiple_of((my_z ^ dz) * N, N), N), :] = ref[...]
+    for z in range(4):
+        parts = []
+        for j in range(16):
+            dx = my_x ^ (j // 4)
+            slot = 4 * (j % 4) + (dx ^ (dx // 2))
+            parts.append(v_ref[pl.ds(slot * 32 + z, 8, stride=4), :])
+        v = jnp.concatenate(parts, axis=0)
+        v = jnp.concatenate([v, v], axis=0)
+        s = s_ref[:, 2 * N * z : 2 * N * (z + 1)] * jnp.concatenate([v, v], axis=1)
         hi, lo = split(s)
         g = mm(xf_ref[...], hi) + mm(xf_ref[...], lo) + mm(xfl_ref[...], hi)
         rows = jnp.concatenate(
@@ -186,7 +201,8 @@
             axis=0,
         )
         hi, lo = split(rows)
-        out = mm(hi, yf_ref[...]) + mm(lo, yf_ref[...]) + mm(hi, yfl_ref[...])
+        both = mm(hi, yf_ref[...])
+        out = both[:, :N] + both[:, N:] + mm(lo, yf_ref[:, :N])
         for b in range(2):
             p = 4 * b + z
             o_ref[pl.ds(p, H, stride=8), :] = out[b * K : b * K + H]
@@ -194,39 +210,32 @@
     o_ref[8 * H : 8 * (N - H), :] = jnp.zeros((8 * (N - K), N), F32)
 
 
-def update_kernel(
-    r_ref, wave_ref, previous_ref, extent_ref, zh_ref, zl_ref, metric_ref, center_ref, half_ref, o_ref
-):
+def update_kernel(r_ref, wave_ref, previous_ref, aux_ref, zh_ref, zl_ref, o_ref):
     outer = outer_lanes((K, N))
     sign = jnp.where(outer, -1.0, 1.0)
-    size = kept_abs((K, N))
+    size = kept_abs((K, N)).astype(F32)
     two_pi = 2.0 * math.pi
     lane = lax.broadcasted_iota(jnp.int32, (K, N), 1)
     signed_y = jnp.where(lane < N // 2, lane, lane - N)
     kinetic_y = (two_pi * signed_y.astype(F32) / N) ** 2
-    kinetic_z = (two_pi * size.astype(F32) / N) ** 2
-    factor = 2.0 / half_ref[0]
-    center = center_ref[0]
+    kinetic_z = (two_pi * size / N) ** 2
+    kinetic_zy = aux_ref[7:8, :] * kinetic_z + aux_ref[6:7, :] * kinetic_y
+    center, factor = aux_ref[4:5, :], aux_ref[8:9, :]
     zeros = jnp.zeros((N - K, N), F32)
     for gx in range(4):
         hi, lo = split(r_ref[:, 8 * gx : 8 * gx + 8, :].reshape(2 * N, N))
         pq = mm(zh_ref[...], hi) + mm(zh_ref[...], lo) + mm(zl_ref[...], hi)
-        keep = size <= extent_ref[gx : gx + 1, :]
+        keep = size <= aux_ref[gx : gx + 1, :]
         index_x = jnp.full((K, N), lax.axis_index("fft") * 4 + gx, jnp.int32)
         signed_x = jnp.where(index_x < N // 2, index_x, index_x - N)
         kinetic_x = (two_pi * signed_x.astype(F32) / N) ** 2
-        kinetic = 0.5 * (
-            metric_ref[0] * kinetic_x + metric_ref[2] * kinetic_z + metric_ref[1] * kinetic_y
-        )
+        scale = 0.5 * (aux_ref[5:6, :] * kinetic_x + kinetic_zy) - center
         for b in range(2):
             p, q = pq[b * K : b * K + K], pq[2 * K + b * K : 2 * K + b * K + K]
             applied = p - pltpu.roll(q, N // 2, 1) * sign
             for part, term in ((0, applied), (1, pltpu.roll(applied, N // 2, 1))):
-                c = kept_rows(wave_ref, part, b, gx)
-                value = factor * (kinetic * c + term - center * c) - kept_rows(
-                    previous_ref, part, b, gx
-                )
-                value = jnp.where(keep, value, 0.0)
+                value = factor * (scale * kept_rows(wave_ref, part, b, gx) + term)
+                value = jnp.where(keep, value - kept_rows(previous_ref, part, b, gx), 0.0)
                 o_ref[part, b, gx, 0:H, :] = value[:H]
                 o_ref[part, b, gx, H : N - H, :] = zeros
                 o_ref[part, b, gx, N - H : N, :] = value[H:]
@@ -237,15 +246,15 @@
 HBM = pl.BlockSpec(memory_space=pltpu.HBM)
 
 
-def call(kernel, shape, specs, flops, scratch=()):
+def call(kernel, shape, specs, flops, scratch=(), limit=16 << 20):
     return pl.pallas_call(
         kernel,
-        out_shape=jax.ShapeDtypeStruct(shape, F32),
+        out_shape=[jax.ShapeDtypeStruct(one, F32) for one in shape],
         in_specs=specs,
-        out_specs=VMEM,
+        out_specs=[VMEM] * len(shape),
         scratch_shapes=list(scratch),
         cost_estimate=pl.CostEstimate(flops=flops, bytes_accessed=2 << 20, transcendentals=0),
-        compiler_params=pltpu.CompilerParams(vmem_limit_bytes=16 << 20),
+        compiler_params=pltpu.CompilerParams(vmem_limit_bytes=limit),
     )
 
 
@@ -259,17 +268,16 @@
 
 
 def gather_potential(potential):
-    near = potential.reshape(32, N)
-    for dx, dz in ((0, 1), (0, 3), (1, 0)):
-        near = jnp.concatenate([near, exchange(near, dx, dz)], axis=0)
-    return near, exchange(near, 3, 0)
+    line = potential.reshape(32, N)
+    for dx in (1, 3):
+        line = jnp.concatenate([line, exchange(line, dx, 0)], axis=0)
+    return [line] + [exchange(line, 0, dz) for dz in (1, 3, 2)]
 
 
 def local(wave, previous, potential, column_extent, metric, center, halfwidth):
     zi, zf = split_table(z_inverse_table()), split_table(z_forward_table())
     yi, yf = split_table(y_inverse_table()), split_table(y_forward_table())
     xi, xf = split_table(x_inverse_table()), split_table(x_forward_table())
-    near, far = gather_potential(potential)
     scratch = [
         pltpu.VMEM((2, 2, 4, K, N), F32),
         pltpu.VMEM((4, N), jnp.int32),
@@ -277,17 +285,32 @@
         pltpu.VMEM((2 * N, 4 * K), BF16),
         pltpu.SemaphoreType.DMA((5,)),
     ]
-    blocks = call(z_inverse_kernel, (32, 32, N), [HBM] * 4, 200_000_000, scratch)(
+    (blocks,) = call(z_inverse_kernel, [(32, 32, N)], [HBM] * 4, 200_000_000, scratch, 63 << 20)(
         wave, column_extent, *zi
     )
+    pieces = gather_potential(potential)
     blocks = swap(blocks).reshape(1024, N)
-    blocks = call(middle_kernel, (1024, N), [VMEM] * 11, 800_000_000)(
-        blocks, near, far, *yi, *xi, *xf, *yf
-    )
+    shapes = [(2 * N, 8 * N), (16, N)]
+    field, aux = call(inverse_kernel, shapes, [VMEM] * 6 + [SMEM] * 3, 400_000_000)(
+        blocks,
+        np.concatenate([yi[0], yi[0]], axis=0),
+        yi[1],
+        np.concatenate([xi[0], xi[0]], axis=1),
+        xi[1],
+        column_extent,
+        metric,
+        center,
+        halfwidth,
+    )
+    scratch = [pltpu.VMEM((4 * N, N), F32)]
+    (blocks,) = call(
+        forward_kernel, [(1024, N)], [VMEM] * 8, 400_000_000, scratch
+    )(field, *pieces, *xf, np.concatenate(yf, axis=1))
     blocks = swap(blocks.reshape(32, 32, N))
-    return call(update_kernel, wave.shape, [VMEM] * 6 + [SMEM] * 3, 200_000_000)(
-        blocks, wave, previous, column_extent, *zf, metric, center, halfwidth
-    )
+    (out,) = call(update_kernel, [wave.shape], [VMEM] * 6, 200_000_000)(
+        blocks, wave, previous, aux, *zf
+    )
+    return out
 
 
 def solution(mesh):

time: 82.1 us -> 77.2 us (0.940)
  blocking collectives: 0 us -> 27.6 us
  waiting for transfers between devices: 22.5 us -> 5.74 us
  starting transfers between devices: 45.3 us -> 34.1 us
  local copies, waits for them, and re-layouts: 3.8 us -> 0.66 us
  Pallas kernels: 8.37 us -> 7.06 us
    all_to_all x0 -> x1, blocking collectives: none -> 27.6 us  [swap(): lax.all_to_all(blocks, 'fft', split_axis=0, concat_axis=0, tiled=True)]
    all_to_all x2 -> x1, waiting for transfers between devices: 15.2 us -> 0.01 us  [swap(): lax.all_to_all(blocks, 'fft', split_axis=0, concat_axis=0, tiled=True)]
    all_to_all x2 -> x1, starting transfers between devices: 22.3 us -> 10.7 us  [swap(): lax.all_to_all(blocks, 'fft', split_axis=0, concat_axis=0, tiled=True)]
    unnamed x38 -> x28, local copies, waits for them, and re-layouts: 3.8 us -> 0.66 us
    ppermute x4 -> x5, waiting for transfers between devices: 7.25 us -> 5.74 us  [exchange(): return lax.ppermute(value, 'band', pairs)]
    pallas_call x3 -> x4, Pallas kernels: 8.37 us -> 7.06 us  [the longest x1 2.67 us: local(): call(z_inverse_kernel, [(32, 32, N)], [HBM] * 4, 200000000, scratch, 63 <...]
    ppermute x4 -> x5, starting transfers between devices: 22.9 us -> 23.4 us  [exchange(): return lax.ppermute(value, 'band', pairs)]
  transfers between devices with their start and end apart: 6 -> 6, of which waited for: 5 -> 3; matrix products, arithmetic and copies ran while one was open for 0% -> 0% of each run, Pallas kernels for 0% -> 2%
where the time goes in v1:
time: 77.2 us; the launch traced here: 76.8 us
  starting transfers between devices  34.1 us (44%)
  blocking collectives  27.6 us (36%)
  Pallas kernels  7.06 us (9%)
  waiting for transfers between devices  5.74 us (7%)
  between operations  1.54 us (2%)
    all_to_all x1, blocking collectives, swap(): lax.all_to_all(blocks, 'fft', split_axis=0, concat_axis=0, tiled=True)  27.6 us
    ppermute x5, starting transfers between devices, exchange(): return lax.ppermute(value, 'band', pairs)  23.4 us
    all_to_all x1, starting transfers between devices, swap(): lax.all_to_all(blocks, 'fft', split_axis=0, concat_axis=0, tiled=True)  10.7 us
    ppermute x5, waiting for transfers between devices, exchange(): return lax.ppermute(value, 'band', pairs)  5.74 us
    pallas_call x1, Pallas kernels, local(): call(z_inverse_kernel, [(32, 32, N)], [HBM] * 4, 200000000, scratch, 63 <...  2.67 us
    pallas_call x1, Pallas kernels, local(): call(update_kernel, [wave.shape], [VMEM] * 6, 200000000)  1.7 us
  transfers between devices with their start and end apart: 6, of which 3 were waited for; matrix products, arithmetic and copies ran while one was open for 0% of the time, Pallas kernels for 2%

profile of v1, /device:TPU:1, one launch (start us, length us, event | category | flops | bytes accessed | tf_op | source)
XLA Modules:
  0.0 76.8 jit_solution(6706687830265856665)
XLA Ops:
  0.0 2.7 %shard_map.172 = f32[32,32,128]{2,1,0:T(8,128)} custom-call(f32[2,2,4,128,128]{4,3,2,1,0:T(8,128)} %wave_ref.1, s32[4,128]{1,0:T(4,128)} %extent_ref.1, bf16[256,256]{1,0:T(8,128)(2,1)} %constant.22.clone.th_hbm, bf16[256,256]{1,0:T(8,128)(2,1)} %constant.23.clone.tl_hbm), custom_call_target="tpu_custom_call" | custom-call | flops 200000000 | bytes 2097152 | tf_op jit(solution)/shard_map/pallas_call | solution.py:288
  2.7 0.0 copy-start.13
  2.7 0.0 copy-start.10
  2.7 0.0 copy-start.12
  2.7 10.7 %all-to-all-start = ((f32[32,32,128]{2,1,0:T(8,128)}), f32[32,32,128]{2,1,0:T(8,128)S(1)}, u32[]{:S(2)}, u32[]{:S(2)}) async-start(f32[32,32,128]{2,1,0:T(8,128)} %shard_map.172), calls=%async_computation | async-start | bytes 1048576 | tf_op jit(solution)/shard_map/all_to_all | solution.py:262
  13.4 0.0 copy-start.9
  13.4 0.0 copy-done.13
  13.5 3.3 %collective-permute-start = (f32[32,128]{1,0:T(8,128)S(1)}, f32[32,128]{1,0:T(8,128)S(1)}, u32[]{:S(2)}, u32[]{:S(2)}) collective-permute-start(f32[32,128]{1,0:T(8,128)S(1)} %bitcast.5), channel_id=1, source_target_pairs={{0,128},{32,160},{64,192},{96,224},{128,0},{160,32},{192,64},{224,... | collective-permute-start | bytes 49160 | tf_op jit(solution)/shard_map/ppermute | solution.py:267
  16.7 1.6 %collective-permute-done = f32[32,128]{1,0:T(8,128)S(1)} collective-permute-done((f32[32,128]{1,0:T(8,128)S(1)}, f32[32,128]{1,0:T(8,128)S(1)}, u32[]{:S(2)}, u32[]{:S(2)}) %collective-permute-start) | collective-permute-done | bytes 16416 | tf_op jit(solution)/shard_map/ppermute | solution.py:267
  18.4 0.0 copy-start.11
  18.4 4.5 %collective-permute-start.1 = (f32[64,128]{1,0:T(8,128)S(1)}, f32[64,128]{1,0:T(8,128)S(1)}, u32[]{:S(2)}, u32[]{:S(2)}) collective-permute-start(f32[64,128]{1,0:T(8,128)S(1)} %pad_maximum_fusion.1), channel_id=1, source_target_pairs={{0,384},{32,416},{64,448},{96,480},{128,256},{160,288},{192,320},{... | collective-permute-start | bytes 98312 | tf_op jit(solution)/shard_map/ppermute | solution.py:267
  22.9 1.8 %collective-permute-done.1 = f32[64,128]{1,0:T(8,128)S(1)} collective-permute-done((f32[64,128]{1,0:T(8,128)S(1)}, f32[64,128]{1,0:T(8,128)S(1)}, u32[]{:S(2)}, u32[]{:S(2)}) %collective-permute-start.1) | collective-permute-done | bytes 32800 | tf_op jit(solution)/shard_map/ppermute | solution.py:267
  24.7 5.8 %collective-permute-start.2 = (f32[128,128]{1,0:T(8,128)S(1)}, f32[128,128]{1,0:T(8,128)S(1)}, u32[]{:S(2)}, u32[]{:S(2)}) collective-permute-start(f32[128,128]{1,0:T(8,128)S(1)} %pad_maximum_fusion.v0_ref), channel_id=1, source_target_pairs={{0,32},{32,0},{64,96},{96,64},{128,160},{160,128},{192,224},{224,1... | collective-permute-start | bytes 196616 | tf_op jit(solution)/shard_map/ppermute | solution.py:267
  30.5 6.1 %collective-permute-start.3 = (f32[128,128]{1,0:T(8,128)S(1)}, f32[128,128]{1,0:T(8,128)S(1)}, u32[]{:S(2)}, u32[]{:S(2)}) collective-permute-start(f32[128,128]{1,0:T(8,128)S(1)} %pad_maximum_fusion.v0_ref), channel_id=1, source_target_pairs={{0,96},{32,64},{64,32},{96,0},{128,224},{160,192},{192,160},{224,1... | collective-permute-start | bytes 196616 | tf_op jit(solution)/shard_map/ppermute | solution.py:267
  36.6 3.7 %collective-permute-start.4 = (f32[128,128]{1,0:T(8,128)S(1)}, f32[128,128]{1,0:T(8,128)S(1)}, u32[]{:S(2)}, u32[]{:S(2)}) collective-permute-start(f32[128,128]{1,0:T(8,128)S(1)} %pad_maximum_fusion.v0_ref), channel_id=1, source_target_pairs={{0,64},{32,96},{64,0},{96,32},{128,192},{160,224},{192,128},{224,1... | collective-permute-start | bytes 196616 | tf_op jit(solution)/shard_map/ppermute | solution.py:267
  41.0 0.0 copy-start.7
  41.7 0.0 copy-start.8
  41.7 0.0 all-to-all-done
  41.7 0.0 copy-done.10
  41.7 0.0 copy-done.12
  41.7 0.0 copy-done.9
  41.7 0.0 copy-done.11
  41.7 0.0 copy-done.7
  41.7 0.6 copy-done.8
  42.3 0.0 copy-start.4
  42.3 0.0 copy-start.5
  42.3 0.0 copy-start.6
  42.3 1.4 %shard_map.173 = (f32[256,1024]{1,0:T(8,128)S(1)}, f32[16,128]{1,0:T(8,128)S(1)}) custom-call(f32[1024,128]{1,0:T(8,128)S(1)} %bitcast.4, bf16[256,256]{1,0:T(8,128)(2,1)S(1)} %copy-done.9, bf16[128,256]{1,0:T(8,128)(2,1)S(1)} %copy-done.11, bf16[256,256]{1,0:T(8,128)(2,1)S(1)} %copy-done.10, bf16[256,128]{1,0:T(8,128)(2,1)S(1)} %copy-done.12, ...), custom_call_target="tpu_custom_call" | custom-call | flops 400000000 | bytes 2097152 | tf_op jit(solution)/shard_map/pallas_call | solution.py:294
  43.7 0.0 collective-permute-done.2.v1_ref
  43.7 0.0 collective-permute-done.3.v3_ref
  43.7 2.3 %collective-permute-done.4.v2_ref = f32[128,128]{1,0:T(8,128)S(1)} collective-permute-done((f32[128,128]{1,0:T(8,128)S(1)}, f32[128,128]{1,0:T(8,128)S(1)}, u32[]{:S(2)}, u32[]{:S(2)}) %collective-permute-start.4) | collective-permute-done | bytes 65568 | tf_op jit(solution)/shard_map/ppermute | solution.py:267
  46.1 0.0 copy-done.4
  46.1 0.0 copy-done.5
  46.1 0.0 copy-done.6
  46.1 0.0 copy-start.1
  46.1 0.0 copy-start.2
  46.1 0.0 copy-start.3
  46.1 1.3 %shard_map.174 = f32[1024,128]{1,0:T(8,128)S(1)} custom-call(f32[256,1024]{1,0:T(8,128)S(1)} %get-tuple-element.7.s_ref, f32[128,128]{1,0:T(8,128)S(1)} %pad_maximum_fusion.v0_ref, f32[128,128]{1,0:T(8,128)S(1)} %collective-permute-done.2.v1_ref, f32[128,128]{1,0:T(8,128)S(1)} %collective-permute-done.3.v3_ref, ...), custom_call_target="tpu_custom_call" | custom-call | flops 400000000 | bytes 2097152 | tf_op jit(solution)/shard_map/pallas_call | solution.py:306
  47.4 0.0 copy-start
  47.4 27.6 %all_to_all.10.r_ref = f32[32,32,128]{2,1,0:T(8,128)S(1)} all-to-all(f32[32,32,128]{2,1,0:T(8,128)S(1)} %bitcast.3), channel_id=1, replica_groups=mesh['band'=16,'fft'=32] {'fft'}, dimensions={0} | all-to-all | bytes 1048576 | tf_op jit(solution)/shard_map/all_to_all | solution.py:262
  75.0 0.0 copy-done.1
  75.0 0.0 copy-done.2
  75.0 0.0 copy-done.3
  75.1 0.0 copy-done
  75.1 1.7 %shard_map.175 = f32[2,2,4,128,128]{4,3,2,1,0:T(8,128)} custom-call(f32[32,32,128]{2,1,0:T(8,128)S(1)} %all_to_all.10.r_ref, f32[2,2,4,128,128]{4,3,2,1,0:T(8,128)S(1)} %copy-done, f32[2,2,4,128,128]{4,3,2,1,0:T(8,128)S(1)} %copy-done.1, f32[16,128]{1,0:T(8,128)S(1)} %get-tuple-element.8.aux_ref, bf16[256,256]{1,0:T(8,128)(2,1)S(1)} %copy-done.2, ...), custom_call_target="tpu_custom_call" | custom-call | flops 200000000 | bytes 2097152 | tf_op jit(solution)/shard_map/pallas_call | solution.py:310
  (2 shorter events, 0.0 us)
Async XLA Ops:
  2.7 10.8 %copy-start.13 = (f32[8,4,128]{2,1,0:T(4,128)S(1)}, f32[8,4,128]{2,1,0:T(4,128)}, u32[]{:S(2)}) copy-start(f32[8,4,128]{2,1,0:T(4,128)} %param.20) | copy-start | bytes 49156
  2.7 39.0 %copy-start.10 = (bf16[256,256]{1,0:T(8,128)(2,1)S(1)}, bf16[256,256]{1,0:T(8,128)(2,1)}, u32[]{:S(2)}) copy-start(bf16[256,256]{1,0:T(8,128)(2,1)} %constant.26.clone.xi_ref) | copy-start | bytes 393220
  2.7 39.0 %copy-start.12 = (bf16[256,128]{1,0:T(8,128)(2,1)S(1)}, bf16[256,128]{1,0:T(8,128)(2,1)}, u32[]{:S(2)}) copy-start(bf16[256,128]{1,0:T(8,128)(2,1)} %constant.27.clone.xil_ref) | copy-start | bytes 196612
  2.7 39.0 %all-to-all-start = ((f32[32,32,128]{2,1,0:T(8,128)}), f32[32,32,128]{2,1,0:T(8,128)S(1)}, u32[]{:S(2)}, u32[]{:S(2)}) async-start(f32[32,32,128]{2,1,0:T(8,128)} %shard_map.172), calls=%async_computation | async-start | bytes 1048576 | tf_op jit(solution)/shard_map/all_to_all | solution.py:262
  13.4 28.3 %copy-start.9 = (bf16[256,256]{1,0:T(8,128)(2,1)S(1)}, bf16[256,256]{1,0:T(8,128)(2,1)}, u32[]{:S(2)}) copy-start(bf16[256,256]{1,0:T(8,128)(2,1)} %constant.24.clone.yi_ref) | copy-start | bytes 393220
  13.5 4.9 %collective-permute-start = (f32[32,128]{1,0:T(8,128)S(1)}, f32[32,128]{1,0:T(8,128)S(1)}, u32[]{:S(2)}, u32[]{:S(2)}) collective-permute-start(f32[32,128]{1,0:T(8,128)S(1)} %bitcast.5), channel_id=1, source_target_pairs={{0,128},{32,160},{64,192},{96,224},{128,0},{160,32},{192,64},{224,... | collective-permute-start | bytes 49160 | tf_op jit(solution)/shard_map/ppermute | solution.py:267
  18.4 23.3 %copy-start.11 = (bf16[128,256]{1,0:T(8,128)(2,1)S(1)}, bf16[128,256]{1,0:T(8,128)(2,1)}, u32[]{:S(2)}) copy-start(bf16[128,256]{1,0:T(8,128)(2,1)} %constant.25.clone.yil_ref) | copy-start | bytes 196612
  18.4 6.3 %collective-permute-start.1 = (f32[64,128]{1,0:T(8,128)S(1)}, f32[64,128]{1,0:T(8,128)S(1)}, u32[]{:S(2)}, u32[]{:S(2)}) collective-permute-start(f32[64,128]{1,0:T(8,128)S(1)} %pad_maximum_fusion.1), channel_id=1, source_target_pairs={{0,384},{32,416},{64,448},{96,480},{128,256},{160,288},{192,320},{... | collective-permute-start | bytes 98312 | tf_op jit(solution)/shard_map/ppermute | solution.py:267
  24.7 19.1 %collective-permute-start.2 = (f32[128,128]{1,0:T(8,128)S(1)}, f32[128,128]{1,0:T(8,128)S(1)}, u32[]{:S(2)}, u32[]{:S(2)}) collective-permute-start(f32[128,128]{1,0:T(8,128)S(1)} %pad_maximum_fusion.v0_ref), channel_id=1, source_target_pairs={{0,32},{32,0},{64,96},{96,64},{128,160},{160,128},{192,224},{224,1... | collective-permute-start | bytes 196616 | tf_op jit(solution)/shard_map/ppermute | solution.py:267
  30.5 13.3 %collective-permute-start.3 = (f32[128,128]{1,0:T(8,128)S(1)}, f32[128,128]{1,0:T(8,128)S(1)}, u32[]{:S(2)}, u32[]{:S(2)}) collective-permute-start(f32[128,128]{1,0:T(8,128)S(1)} %pad_maximum_fusion.v0_ref), channel_id=1, source_target_pairs={{0,96},{32,64},{64,32},{96,0},{128,224},{160,192},{192,160},{224,1... | collective-permute-start | bytes 196616 | tf_op jit(solution)/shard_map/ppermute | solution.py:267
  36.6 9.5 %collective-permute-start.4 = (f32[128,128]{1,0:T(8,128)S(1)}, f32[128,128]{1,0:T(8,128)S(1)}, u32[]{:S(2)}, u32[]{:S(2)}) collective-permute-start(f32[128,128]{1,0:T(8,128)S(1)} %pad_maximum_fusion.v0_ref), channel_id=1, source_target_pairs={{0,64},{32,96},{64,0},{96,32},{128,192},{160,224},{192,128},{224,1... | collective-permute-start | bytes 196616 | tf_op jit(solution)/shard_map/ppermute | solution.py:267
  41.0 0.7 copy-start.7
  41.7 0.7 copy-start.8
  42.3 3.7 %copy-start.4 = (bf16[256,256]{1,0:T(8,128)(2,1)S(1)}, bf16[256,256]{1,0:T(8,128)(2,1)}, u32[]{:S(2)}) copy-start(bf16[256,256]{1,0:T(8,128)(2,1)} %constant.30.clone.yf_ref) | copy-start | bytes 393220
  42.3 3.8 %copy-start.5 = (bf16[128,256]{1,0:T(8,128)(2,1)S(1)}, bf16[128,256]{1,0:T(8,128)(2,1)}, u32[]{:S(2)}) copy-start(bf16[128,256]{1,0:T(8,128)(2,1)} %constant.28.clone.xf_ref) | copy-start | bytes 196612
  42.3 3.8 %copy-start.6 = (bf16[128,256]{1,0:T(8,128)(2,1)S(1)}, bf16[128,256]{1,0:T(8,128)(2,1)}, u32[]{:S(2)}) copy-start(bf16[128,256]{1,0:T(8,128)(2,1)} %constant.29.clone.xfl_ref) | copy-start | bytes 196612
  46.1 29.0 %copy-start.1 = (f32[2,2,4,128,128]{4,3,2,1,0:T(8,128)S(1)}, f32[2,2,4,128,128]{4,3,2,1,0:T(8,128)}, u32[]{:S(2)}) copy-start(f32[2,2,4,128,128]{4,3,2,1,0:T(8,128)} %previous_ref.1) | copy-start | bytes 3145732
  46.1 29.0 %copy-start.2 = (bf16[256,256]{1,0:T(8,128)(2,1)S(1)}, bf16[256,256]{1,0:T(8,128)(2,1)}, u32[]{:S(2)}) copy-start(bf16[256,256]{1,0:T(8,128)(2,1)} %constant.31.clone.zh_ref) | copy-start | bytes 393220
  46.1 29.0 %copy-start.3 = (bf16[256,256]{1,0:T(8,128)(2,1)S(1)}, bf16[256,256]{1,0:T(8,128)(2,1)}, u32[]{:S(2)}) copy-start(bf16[256,256]{1,0:T(8,128)(2,1)} %constant.32.clone.zl_ref) | copy-start | bytes 393220
  47.4 27.7 %copy-start = (f32[2,2,4,128,128]{4,3,2,1,0:T(8,128)S(1)}, f32[2,2,4,128,128]{4,3,2,1,0:T(8,128)}, u32[]{:S(2)}) copy-start(f32[2,2,4,128,128]{4,3,2,1,0:T(8,128)} %wave_ref.1) | copy-start | bytes 3145732
